TPU v7x, 64 devices: a 2x2x8 block of a 4x4x8 slice. The times are simulated.
64 devices in a mesh: rep: 4 (over x, y), dp: 16 (over z, core).
Axes of the slice: x: 2, y: 2, z: 8, core: 2. Of those that a mesh axis runs over, the one named last changes fastest.
The devices are a block of a 4x4x8 slice.
Arguments:
- g_w_gate: bfloat16 [64, 2, 1024, 2816], P(('rep', 'dp')), parts along dimension 0
- g_w_up: bfloat16 [64, 2, 1024, 2816], P(('rep', 'dp')), parts along dimension 0
- g_w_down: bfloat16 [64, 2, 2816, 1024], P(('rep', 'dp')), parts along dimension 0
- w_gate: bfloat16 [2, 1024, 2816], replicated
- w_up: bfloat16 [2, 1024, 2816], replicated
- w_down: bfloat16 [2, 2816, 1024], replicated
- m_w_gate: float32 [2, 1024, 2816], P(None, 'dp')
- m_w_up: float32 [2, 1024, 2816], P(None, 'dp')
- m_w_down: float32 [2, 2816, 1024], P(None, 'dp')
- v_w_gate: float32 [2, 1024, 2816], P(None, 'dp')
- v_w_up: float32 [2, 1024, 2816], P(None, 'dp')
- v_w_down: float32 [2, 2816, 1024], P(None, 'dp')
Outputs:
- output 1: bfloat16 [8, 1024, 2816], P('rep'), parts along dimension 0
- output 2: bfloat16 [8, 1024, 2816], P('rep'), parts along dimension 0
- output 3: bfloat16 [8, 2816, 1024], P('rep'), parts along dimension 0
- output 4: float32 [8, 1024, 2816], P('rep', 'dp'), parts along dimension 0
- output 5: float32 [8, 1024, 2816], P('rep', 'dp'), parts along dimension 0
- output 6: float32 [8, 2816, 1024], P('rep', 'dp'), parts along dimension 0
- output 7: float32 [8, 1024, 2816], P('rep', 'dp'), parts along dimension 0
- output 8: float32 [8, 1024, 2816], P('rep', 'dp'), parts along dimension 0
- output 9: float32 [8, 2816, 1024], P('rep', 'dp'), parts along dimension 0
There are 4 independent parts. A program takes and returns all parts, laid end to end along the dimension named above; an argument that names none is the same for every part.
All inputs are finite; a program needn't handle non-finite values.
Results may differ from a plain program's by a relative error of at most 0.022.
Values are sent between devices in bfloat16 or wider.
A program may use at most 768 MiB of HBM per device.

v0:
```python
import jax
import jax.numpy as jnp
from jax import lax
from jax.sharding import PartitionSpec as P


def adamw(w, m, v, g):
    m = 0.9 * m + 0.1 * g
    v = 0.95 * v + 0.05 * g * g
    step = m * lax.rsqrt(v + 1e-8) + 0.1 * w
    return (w - 0.02 * step).astype(jnp.bfloat16), m, v


def clipped(gradients, sum_of_squares, count):
    factor = jnp.minimum(1.0, 0.5 * lax.rsqrt(sum_of_squares / count + 1e-30))
    return [g * factor for g in gradients]


def solution(mesh):
    def step(*arrays):
        terms, weights, m, v = (arrays[i : i + 3] for i in (0, 3, 6, 9))
        gradients = [lax.psum_scatter(t[0], "dp", scatter_dimension=1, tiled=True).astype(jnp.float32) for t in terms]
        squares = lax.psum(sum(jnp.sum(g * g) for g in gradients), "dp")
        gradients = clipped(gradients, squares, lax.psum(1, "dp") * sum(g.size for g in gradients))
        me = lax.axis_index("dp")
        own = [lax.dynamic_slice_in_dim(w, me * one.shape[1], one.shape[1], 1).astype(jnp.float32) for w, one in zip(weights, m, strict=True)]
        new = [adamw(w, m, v, g) for w, m, v, g in zip(own, m, v, gradients, strict=True)]
        whole = [lax.all_gather(one[0], "dp", axis=1, tiled=True) for one in new]
        return (*whole, *(one[1] for one in new), *(one[2] for one in new))

    all_of, cut = P(None, None, None), P(None, "dp", None)
    return jax.shard_map(
        step,
        mesh=mesh,
        in_specs=(P(("rep", "dp"), None, None, None),) * 3 + (all_of,) * 3 + (cut,) * 6,
        out_specs=(P("rep", None, None),) * 3 + (P("rep", "dp", None),) * 6,
        check_vma=False,
    )
```

profile of v0, /device:TPU:21, one launch (start us, length us, event | category | flops | bytes accessed | tf_op | source)
XLA Modules:
  0.0 506.1 jit_solution(10648199629315563579)
XLA Ops:
  7.2 0.1 reduce-scatter.4.cloned.1.call-start
  7.3 0.7 reduce-scatter.4.cloned.1.call-update
  8.0 0.1 reduce-scatter.6.cloned.1.call-start
  8.1 0.7 reduce-scatter.6.cloned.1.call-update
  8.8 0.1 reduce-scatter.8.cloned.1.call-start
  8.9 0.7 reduce-scatter.8.cloned.1.call-update
  9.6 0.0 copy-start.3
  9.6 0.1 all-gather.8.cloned.1.call-start
  9.7 76.2 %reduce-scatter.4.cloned.1.call-done = bf16[2,64,2816]{2,1,0:T(8,128)(2,1)} async-done(((bf16[2,1024,2816]{2,1,0:T(8,128)(2,1)}), bf16[2,64,2816]{2,1,0:T(8,128)(2,1)}) %reduce-scatter.4.cloned.1.call-update) | async-done | bytes 720912 | tf_op jit(solution)/shard_map/reduce_scatter | solution.py:22
  85.9 2.1 fusion.9
  88.0 73.1 %reduce-scatter.6.cloned.1.call-done = bf16[2,64,2816]{2,1,0:T(8,128)(2,1)} async-done(((bf16[2,1024,2816]{2,1,0:T(8,128)(2,1)}), bf16[2,64,2816]{2,1,0:T(8,128)(2,1)}) %reduce-scatter.6.cloned.1.call-update) | async-done | bytes 720912 | tf_op jit(solution)/shard_map/reduce_scatter | solution.py:22
  161.0 2.1 fusion.10
  164.4 71.8 %reduce-scatter.8.cloned.1.call-done = bf16[2,176,1024]{2,1,0:T(8,128)(2,1)} async-done(((bf16[2,2816,1024]{2,1,0:T(8,128)(2,1)}), bf16[2,176,1024]{2,1,0:T(8,128)(2,1)}) %reduce-scatter.8.cloned.1.call-update) | async-done | bytes 720912 | tf_op jit(solution)/shard_map/reduce_scatter | solution.py:22
  236.2 2.1 fusion.11
  239.0 26.5 %psum.7 = f32[]{:T(128)} all-reduce(f32[]{:T(128)S(6)} %add.65), channel_id=1, replica_groups=mesh['rep'=4,'dp'=16] {'dp'}, use_global_device_ids=true, to_apply=%region_6.0 | all-reduce | flops 1 | bytes 8 | tf_op jit(solution)/shard_map/psum | solution.py:23
  266.2 0.0 copy-done.3
  266.2 0.0 copy-start.2
  266.2 4.1 fusion.17
  270.3 0.1 all-gather.8.cloned.1.call-update
  270.4 0.1 all-gather.4.cloned.1.call-start
  270.5 0.0 copy-done.2
  270.5 0.0 copy-start.1
  270.5 4.3 fusion.8
  274.7 0.1 all-gather.4.cloned.1.call-update
  274.8 0.1 all-gather.6.cloned.1.call-start
  274.9 0.0 copy-done.1
  274.9 4.2 fusion.14
  279.1 0.1 all-gather.6.cloned.1.call-update
  279.2 60.2 %all-gather.8.cloned.1.call-done = bf16[2,2816,1024]{2,1,0:T(8,128)(2,1)} async-done(((bf16[2,176,1024]{2,1,0:T(8,128)(2,1)}), bf16[2,2816,1024]{2,1,0:T(8,128)(2,1)}) %all-gather.8.cloned.1.call-update) | async-done | bytes 11534352 | tf_op jit(solution)/shard_map/all_gather | solution.py:28
  339.4 67.9 %all-gather.4.cloned.1.call-done = bf16[2,1024,2816]{2,1,0:T(8,128)(2,1)} async-done(((bf16[2,64,2816]{2,1,0:T(8,128)(2,1)}), bf16[2,1024,2816]{2,1,0:T(8,128)(2,1)}) %all-gather.4.cloned.1.call-update) | async-done | bytes 11534352 | tf_op jit(solution)/shard_map/all_gather | solution.py:28
  407.3 68.0 %all-gather.6.cloned.1.call-done = bf16[2,1024,2816]{2,1,0:T(8,128)(2,1)} async-done(((bf16[2,64,2816]{2,1,0:T(8,128)(2,1)}), bf16[2,1024,2816]{2,1,0:T(8,128)(2,1)}) %all-gather.6.cloned.1.call-update) | async-done | bytes 11534352 | tf_op jit(solution)/shard_map/all_gather | solution.py:28
  475.3 0.0 copy-start
  475.3 0.0 slice-start
  475.3 0.0 slice-start.1
  475.3 11.7 %copy.24 = bf16[2,1024,2816]{2,1,0:T(8,128)(2,1)} copy(bf16[2,1024,2816]{2,1,0:T(8,128)(2,1)} %all-gather.4.cloned.1.call-done) | data formatting | bytes 23068672
  486.9 0.0 copy-done
  486.9 0.0 slice-start.2
  486.9 5.8 %copy.25 = bf16[2,1024,2816]{2,1,0:T(8,128)(2,1)} copy(bf16[2,1024,2816]{2,1,0:T(8,128)(2,1)S(1)} %copy-done) | data formatting | bytes 23068672
  492.8 0.0 slice-done
  492.8 0.8 slice-done.1
  493.6 1.2 slice-done.2
  494.8 4.4 copy.26
  (1 shorter events, 0.0 us)
Async XLA Ops:
  7.2 78.7 %reduce-scatter.4.cloned.1.call-start = ((), (), s32[]{:S(2)}) async-start(), calls=%async_computation.3 | async-start | bytes 12255232 | tf_op jit(solution)/shard_map/reduce_scatter | solution.py:22
  8.0 153.1 %reduce-scatter.6.cloned.1.call-start = ((), (), s32[]{:S(2)}) async-start(), calls=%async_computation.4 | async-start | bytes 12255232 | tf_op jit(solution)/shard_map/reduce_scatter | solution.py:22
  8.8 227.4 %reduce-scatter.8.cloned.1.call-start = ((), (), s32[]{:S(2)}) async-start(), calls=%async_computation.5 | async-start | bytes 12255232 | tf_op jit(solution)/shard_map/reduce_scatter | solution.py:22
  9.6 256.6 %copy-start.3 = (f32[2,176,1024]{2,1,0:T(8,128)S(1)}, f32[2,176,1024]{2,1,0:T(8,128)}, u32[]{:S(2)}) copy-start(f32[2,176,1024]{2,1,0:T(8,128)} %param.23) | copy-start | bytes 4325380
  9.6 329.8 %all-gather.8.cloned.1.call-start = ((), (), s32[]{:S(2)}) async-start(), calls=%async_computation.8 | async-start | bytes 12255232 | tf_op jit(solution)/shard_map/all_gather | solution.py:28
  266.2 4.3 copy-start.2
  270.4 136.9 %all-gather.4.cloned.1.call-start = ((), (), s32[]{:S(2)}) async-start(), calls=%async_computation.6 | async-start | bytes 12255232 | tf_op jit(solution)/shard_map/all_gather | solution.py:28
  270.5 4.4 copy-start.1
  274.8 200.5 %all-gather.6.cloned.1.call-start = ((), (), s32[]{:S(2)}) async-start(), calls=%async_computation.7 | async-start | bytes 12255232 | tf_op jit(solution)/shard_map/all_gather | solution.py:28
  475.3 11.7 %copy-start = (bf16[2,1024,2816]{2,1,0:T(8,128)(2,1)S(1)}, bf16[2,1024,2816]{2,1,0:T(8,128)(2,1)}, u32[]{:S(2)}) copy-start(bf16[2,1024,2816]{2,1,0:T(8,128)(2,1)} %all-gather.6.cloned.1.call-done) | copy-start | bytes 34603012
  475.3 17.5 %slice-start = ((s8[11534336]{0:T(1024)(128)(4,1)}), s8[4194304]{0:T(1024)(128)(4,1)S(1)}, s32[]{:S(2)}) async-start(s8[11534336]{0:T(1024)(128)(4,1)} %bitcast.6), calls=%async_computation.9 | async-start | bytes 8388608
  475.3 18.3 %slice-start.1 = ((s8[11534336]{0:T(1024)(128)(4,1)}), s8[4194304]{0:T(1024)(128)(4,1)S(1)}, s32[]{:S(2)}) async-start(s8[11534336]{0:T(1024)(128)(4,1)} %bitcast.6), calls=%async_computation.10 | async-start | bytes 8388608
  486.9 7.9 %slice-start.2 = ((s8[11534336]{0:T(1024)(128)(4,1)}), s8[3145728]{0:T(1024)(128)(4,1)S(1)}, s32[]{:S(2)}) async-start(s8[11534336]{0:T(1024)(128)(4,1)} %bitcast.6), calls=%async_computation.11 | async-start | bytes 6291456
Sparse Core Ops, SparseCore 0:
  10.4 75.4 reduce-scatter.3
  88.2 72.7 reduce-scatter.5
  163.4 72.7 reduce-scatter.7
  270.5 68.8 all-gather.7
  341.4 65.8 all-gather.3
  409.4 65.8 all-gather.5
where the time goes:
time: 506 us
  waiting for transfers between devices  420 us (83%)
  blocking collectives  26.5 us (5%)
  local copies, waits for them, and re-layouts  24 us (5%)
  other arithmetic  18.9 us (4%)
  between operations  16.9 us (3%)
    reduce_scatter x3, waiting for transfers between devices, step(): lax.psum_scatter(t[0], 'dp', scatter_dimension=1, tiled=True)  221 us
    all_gather x3, waiting for transfers between devices, step(): whole = [lax.all_gather(one[0], 'dp', axis=1, tiled=True) for one in new]  196 us
    psum x1, blocking collectives, step(): squares = lax.psum(sum((jnp.sum(g * g) for g in gradients)), 'dp')  26.5 us
    unnamed x17, local copies, waits for them, and re-layouts  24 us
    convert_element_type x3, other arithmetic, adamw(): return ((w - 0.02 * step).astype(jnp.bfloat16), m, v)  12.6 us
  transfers between devices with their start and end apart: 6, of which 6 were waited for; matrix products, arithmetic and copies ran while one was open for 2% of the time, Pallas kernels for 0%

commit v1 on v0

v1 whole, which is shorter than its diff:
```python
import functools

import jax
import jax.numpy as jnp
from jax import lax
from jax.experimental import pallas as pl
from jax.experimental.pallas import tpu as pltpu
from jax.sharding import PartitionSpec as P

MESH = pl.DeviceIdType.MESH
CORES = 2
SLAB = 16


def kernel(n, *refs):
    g, w, m_in, v_in = refs[0:3], refs[3:6], refs[6:9], refs[9:12]
    whole, m, v = refs[12:15], refs[15:18], refs[18:21]
    wide_slots, tall_slots, wide_w, tall_w, squares = refs[21:26]
    (load_sem, give_send, give_recv, sum_send, sum_recv, state_sem, norm_send, norm_recv, new_send, new_recv, pass_send, pass_recv) = refs[26:]

    me = lax.axis_index("dp")
    chips = n // CORES
    chip, core = me // CORES, lax.rem(me, CORES)
    partner = {"dp": chip * CORES + (1 - core)}
    ahead = {"dp": lax.rem(chip + 1, chips) * CORES + core}
    behind = {"dp": lax.rem(chip + chips - 1, chips) * CORES + core}
    layers = m[0].shape[0]
    units = [(a, layer) for layer in range(layers) for a in range(3)]
    half = len(units) // 2
    order = [u for pair in zip(range(half), range(half, len(units)), strict=True) for u in pair]
    forward = [u < half for u in range(len(units))]

    def rows(a, block, which):
        size = m[a].shape[1]
        return pl.ds(pl.multiple_of((block * CORES + which) * size, SLAB), size)

    def slot(step, u):
        a, layer = units[u]
        return tall_slots.at[step, layer] if a == 2 else wide_slots.at[step, a * layers + layer]

    def w_own(u):
        a, layer = units[u]
        return tall_w.at[layer] if a == 2 else wide_w.at[a * layers + layer]

    def summed(step, u):
        return lax.rem(chip + 2 * chips - 1 - step, chips) if forward[u] else lax.rem(chip + 1 + step, chips)

    def gathered(step, u):
        return lax.rem(chip + chips - step, chips) if forward[u] else lax.rem(chip + step, chips)

    def remote(src, dst, send, recv, to):
        return pltpu.make_async_remote_copy(src_ref=src, dst_ref=dst, send_sem=send, recv_sem=recv, device_id=to, device_id_type=MESH)

    def load(step, u):
        a, layer = units[u]
        mine = rows(a, summed(step, u), core)
        return pltpu.make_async_copy(g[a].at[0, layer, mine], whole[a].at[layer, mine], load_sem.at[step, u])

    def give(step, u):
        a, layer = units[u]
        block = summed(step, u)
        return remote(
            g[a].at[0, layer, rows(a, block, 1 - core)],
            whole[a].at[layer, rows(a, block, core)],
            give_send.at[step, u],
            give_recv.at[step, u],
            partner,
        )

    def send_sum(step, u):
        a, layer = units[u]
        return remote(
            whole[a].at[layer, rows(a, summed(step, u), core)],
            slot(step, u),
            sum_send.at[step, u],
            sum_recv.at[step, u],
            ahead if forward[u] else behind,
        )

    def send_new(step, u):
        a, layer = units[u]
        mine = whole[a].at[layer, rows(a, gathered(step, u), core)]
        return remote(mine, mine, new_send.at[step, u], new_recv.at[step, u], ahead if forward[u] else behind)

    def pass_new(step, u):
        a, layer = units[u]
        mine = whole[a].at[layer, rows(a, gathered(step, u), core)]
        return remote(mine, mine, pass_send.at[step, u], pass_recv.at[step, u], partner)

    def state(u):
        a, layer = units[u]
        return (
            pltpu.make_async_copy(w[a].at[layer, rows(a, chip, core)], w_own(u), state_sem.at[0, u]),
            pltpu.make_async_copy(m_in[a].at[layer], m[a].at[layer], state_sem.at[1, u]),
            pltpu.make_async_copy(v_in[a].at[layer], v[a].at[layer], state_sem.at[2, u]),
        )

    for u in order:
        load(0, u).start()
    barrier = pltpu.get_barrier_semaphore()
    for other in (partner, ahead, behind):
        pl.semaphore_signal(barrier, inc=1, device_id=other, device_id_type=MESH)
    pl.semaphore_wait(barrier, 3)
    for u in order:
        give(0, u).start()

    def add(step, u, first):
        a, layer = units[u]
        block = summed(step, u)
        size = m[a].shape[1]
        load(step, u).wait()
        give(step, u).wait_recv()
        if not first:
            send_sum(step - 1, u).wait_recv()
        base, other = (block * CORES + core) * size, (block * CORES + 1 - core) * size

        def body(i, squared):
            at = pl.ds(pl.multiple_of(base + i * SLAB, SLAB), SLAB)
            total = whole[a][layer, at, :].astype(jnp.float32)
            total += whole[a][layer, pl.ds(pl.multiple_of(other + i * SLAB, SLAB), SLAB), :].astype(jnp.float32)
            if not first:
                total = slot(step - 1, u)[pl.ds(pl.multiple_of(i * SLAB, SLAB), SLAB), :].astype(jnp.float32) + total
            total = total.astype(jnp.bfloat16)
            whole[a][layer, at, :] = total
            if squared is None:
                return None
            total = total.astype(jnp.float32)
            total = total * total
            pieces = [total[r : r + 8, k : k + 128] for r in range(0, SLAB, 8) for k in range(0, total.shape[1], 128)]
            while len(pieces) > 1:
                pieces = [sum(pieces[k : k + 2]) for k in range(0, len(pieces), 2)]
            return squared + pieces[0]

        return body, size // SLAB

    def add_and_send(step, u, first=False):
        body, count = add(step, u, first)
        lax.fori_loop(0, count, lambda i, _: body(i, None) or 0, 0)
        send_sum(step, u).start()

    def prefetch(step):
        for u in order:
            load(step, u).start()
            give(step, u).start()

    prefetch(1)
    for u in order:
        add_and_send(0, u, first=True)
    for u in order:
        for copy in state(u):
            copy.start()

    def middle(step, carry):
        prefetch(step + 1)
        for u in order:
            add_and_send(step, u)
        return carry

    lax.fori_loop(1, chips - 1, middle, 0)

    total = jnp.zeros((8, 128), jnp.float32)
    for u in order:
        body, count = add(chips - 1, u, False)
        total = lax.fori_loop(0, count, body, total)

    def drained(step, carry):
        for u in order:
            send_sum(step, u).wait_send()
        return carry

    lax.fori_loop(0, chips - 1, drained, 0)

    squares[me] = jnp.sum(total, axis=0, keepdims=True)

    def norm(k):
        return remote(squares.at[me], squares.at[me], norm_send.at[k], norm_recv.at[k], {"dp": lax.rem(me + k, n)})

    for k in range(1, n):
        norm(k).start()
    for u in order:
        for copy in state(u):
            copy.wait()
    for k in range(1, n):
        norm(k).wait_recv()
    every = jnp.sum(jnp.sum(squares[...], axis=0), axis=1, keepdims=True)
    count = n * sum(one.size for one in m)
    factor = jnp.minimum(1.0, 0.5 * lax.rsqrt(every / count + 1e-30))

    for u in order:
        a, layer = units[u]
        base = me * m[a].shape[1]

        def body(i, carry, a=a, layer=layer, u=u, base=base):
            at = pl.ds(pl.multiple_of(i * SLAB, SLAB), SLAB)
            mine = pl.ds(pl.multiple_of(base + i * SLAB, SLAB), SLAB)
            gradient = whole[a][layer, mine, :].astype(jnp.float32) * factor
            weight = w_own(u)[at, :].astype(jnp.float32)
            moment = 0.9 * m[a][layer, at, :] + 0.1 * gradient
            second = 0.95 * v[a][layer, at, :] + 0.05 * gradient * gradient
            m[a][layer, at, :] = moment
            v[a][layer, at, :] = second
            change = moment * lax.rsqrt(second + 1e-8) + 0.1 * weight
            whole[a][layer, mine, :] = (weight - 0.02 * change).astype(jnp.bfloat16)
            return carry

        lax.fori_loop(0, m[a].shape[1] // SLAB, body, 0)
        send_new(0, u).start()
        pass_new(0, u).start()

    def onward(step, carry):
        for u in order:
            send_new(step - 1, u).wait_recv()
            send_new(step, u).start()
            pass_new(step, u).start()
        return carry

    lax.fori_loop(1, chips - 1, onward, 0)
    for u in order:
        send_new(chips - 2, u).wait_recv()
        pass_new(chips - 1, u).start()

    def ended(step, carry):
        for u in order:
            give(step, u).wait_send()
            pass_new(step, u).wait()
        return carry

    lax.fori_loop(0, chips, ended, 0)

    def sent(step, carry):
        for u in order:
            send_new(step, u).wait_send()
        return carry

    lax.fori_loop(0, chips - 1, sent, 0)
    for k in range(1, n):
        norm(k).wait_send()


def write_out(parts, *refs):
    count = (len(refs) - 1) // 2
    copies = []
    for src, dst in zip(refs[:count], refs[count:-1], strict=True):
        layers, size = src.shape[0], src.shape[1] // parts
        for layer in range(layers):
            for part in range(parts):
                at = (layer, pl.ds(part * size, size))
                copies.append(pltpu.make_async_copy(src.at[at], dst.at[at], refs[-1].at[len(copies)]))
    for copy in copies:
        copy.start()
    for copy in copies:
        copy.wait()


def solution(mesh):
    n = mesh.shape["dp"]
    chips = n // CORES

    def step(*arrays):
        weights, m, v = (arrays[i : i + 3] for i in (3, 6, 9))
        layers, wide, columns = m[0].shape
        _, tall, narrow = m[2].shape
        unit = layers * 3
        whole = [pltpu.VMEM(x.shape, x.dtype) for x in weights]
        moments = [pltpu.VMEM(x.shape, x.dtype) for x in (*m, *v)]
        dma = pltpu.SemaphoreType.DMA
        done = pl.pallas_call(
            functools.partial(kernel, n),
            out_shape=[*whole, *moments],
            in_specs=[pl.BlockSpec(memory_space=pltpu.HBM)] * 12,
            out_specs=[pl.BlockSpec(memory_space=pltpu.VMEM)] * 9,
            scratch_shapes=[
                pltpu.VMEM((chips - 1, 2 * layers, wide, columns), jnp.bfloat16),
                pltpu.VMEM((chips - 1, layers, tall, narrow), jnp.bfloat16),
                pltpu.VMEM((2 * layers, wide, columns), jnp.bfloat16),
                pltpu.VMEM((layers, tall, narrow), jnp.bfloat16),
                pltpu.VMEM((n, 1, 128), jnp.float32),
                dma((chips, unit)),
                dma((chips, unit)),
                dma((chips, unit)),
                dma((chips - 1, unit)),
                dma((chips - 1, unit)),
                dma((3, unit)),
                dma((n,)),
                dma((n,)),
                dma((chips - 1, unit)),
                dma((chips - 1, unit)),
                dma((chips, unit)),
                dma((chips, unit)),
            ],
            compiler_params=pltpu.CompilerParams(collective_id=0, has_side_effects=True, vmem_limit_bytes=17 * 2**20),
            name="clipped_step",
        )(*arrays)

        def out(parts, *xs):
            return pl.pallas_call(
                functools.partial(write_out, parts),
                out_shape=[jax.ShapeDtypeStruct(x.shape, x.dtype) for x in xs],
                in_specs=[pl.BlockSpec(memory_space=pltpu.VMEM)] * len(xs),
                out_specs=[pl.BlockSpec(memory_space=pltpu.HBM)] * len(xs),
                scratch_shapes=[dma((len(xs) * layers * parts,))],
                compiler_params=pltpu.CompilerParams(vmem_limit_bytes=2**20),
                name="write_out",
            )(*xs)

        return (*out(4, done[0]), *out(4, done[1]), *out(4, done[2]), *out(1, *done[3:]))

    all_of, cut = P(None, None, None), P(None, "dp", None)
    return jax.shard_map(
        step,
        mesh=mesh,
        in_specs=(P(("rep", "dp"), None, None, None),) * 3 + (all_of,) * 3 + (cut,) * 6,
        out_specs=(P("rep", None, None),) * 3 + (P("rep", "dp", None),) * 6,
        check_vma=False,
    )
```

time: 506 us -> 368 us (0.73)
  waiting for transfers between devices: 420 us -> 0 us
  Pallas kernels: 0 us -> 367 us
  blocking collectives: 26.5 us -> 0 us
  local copies, waits for them, and re-layouts: 24 us -> 0 us
  other arithmetic: 18.9 us -> 0 us
  between operations: 16.9 us -> 0.68 us
    pallas_call x0 -> x5, Pallas kernels: none -> 367 us  [the longest x1 350 us: step(): pl.pallas_call(functools.partial(kernel, n), out_shape=[*whole, *moments]...]
    reduce_scatter x3 -> x0, waiting for transfers between devices: 221 us -> none  [step(): lax.psum_scatter(t[0], 'dp', scatter_dimension=1, tiled=True)]
    all_gather x3 -> x0, waiting for transfers between devices: 196 us -> none  [step(): whole = [lax.all_gather(one[0], 'dp', axis=1, tiled=True) for one in new]]
    psum x1 -> x0, blocking collectives: 26.5 us -> none  [step(): squares = lax.psum(sum((jnp.sum(g * g) for g in gradients)), 'dp')]
    unnamed x17 -> x0, local copies, waits for them, and re-layouts: 24 us -> none
    convert_element_type x3 -> x0, other arithmetic: 12.6 us -> none  [adamw(): return ((w - 0.02 * step).astype(jnp.bfloat16), m, v)]
    reduce_sum x3 -> x0, other arithmetic: 6.26 us -> none  [step(): squares = lax.psum(sum((jnp.sum(g * g) for g in gradients)), 'dp')]
  transfers between devices with their start and end apart: 6 -> 0, of which waited for: 6 -> 0; matrix products, arithmetic and copies ran while one was open for 2% -> 0% of each run, Pallas kernels for 0% -> 0%
where the time goes in v1:
time: 368 us
  Pallas kernels  367 us (100%)
    pallas_call x1, Pallas kernels, step(): pl.pallas_call(functools.partial(kernel, n), out_shape=[*whole, *moments]...  350 us
    pallas_call x4, Pallas kernels, out(): pl.pallas_call(functools.partial(write_out, parts), out_shape=[jax.ShapeD...  16.5 us

profile of v1, /device:TPU:21, one launch (start us, length us, event | category | flops | bytes accessed | tf_op | source)
XLA Modules:
  0.0 367.6 jit_solution(11832487465925905275)
XLA Ops:
  0.6 350.5 %clipped_step.1 = (bf16[2,1024,2816]{2,1,0:T(8,128)(2,1)S(1)}, bf16[2,1024,2816]{2,1,0:T(8,128)(2,1)S(1)}, bf16[2,2816,1024]{2,1,0:T(8,128)(2,1)S(1)}, f32[2,64,...) custom-call(bf16[1,2,1024,2816]{3,2,1,0:T(8,128)(2,1)} %refs_0_.1, ...), custom_call_target="tpu_custom_call" | custom-call | tf_op jit(solution)/shard_map/clipped_step/pallas_call | solution.py:267
  351.1 4.3 %write_out.4 = bf16[2,1024,2816]{2,1,0:T(8,128)(2,1)} custom-call(bf16[2,1024,2816]{2,1,0:T(8,128)(2,1)S(1)} %get-tuple-element.24.refs_0_), custom_call_target="tpu_custom_call" | custom-call | tf_op jit(solution)/shard_map/write_out/pallas_call | solution.py:296
  355.5 3.5 write_out.7
  358.9 4.3 %write_out.5 = bf16[2,1024,2816]{2,1,0:T(8,128)(2,1)} custom-call(bf16[2,1024,2816]{2,1,0:T(8,128)(2,1)S(1)} %get-tuple-element.25.refs_0_), custom_call_target="tpu_custom_call" | custom-call | tf_op jit(solution)/shard_map/write_out/pallas_call | solution.py:296
  363.3 4.3 %write_out.6 = bf16[2,2816,1024]{2,1,0:T(8,128)(2,1)} custom-call(bf16[2,2816,1024]{2,1,0:T(8,128)(2,1)S(1)} %get-tuple-element.26.refs_0_), custom_call_target="tpu_custom_call" | custom-call | tf_op jit(solution)/shard_map/write_out/pallas_call | solution.py:296

commit v2 on v1

v2 whole, which is shorter than its diff:
```python
import functools

import jax
import jax.numpy as jnp
from jax import lax
from jax.experimental import pallas as pl
from jax.experimental.pallas import tpu as pltpu
from jax.sharding import PartitionSpec as P

MESH = pl.DeviceIdType.MESH
CORES = 2
SLAB = 16
TAIL = 48
PIECES = 5
VMEM_LIMIT = 18 * 2**20


def kernel(n, *refs):
    g, w, m_in, v_in = refs[0:3], refs[3:6], refs[6:9], refs[9:12]
    whole, m, v = refs[12:15], refs[15:18], refs[18:21]
    wide_slots, tall_slots, wide_w, tall_w, squares = refs[21:26]
    (load_sem, give_send, give_recv, sum_send, sum_recv, state_sem, norm_send, norm_recv, new_send, new_recv, pass_send, pass_recv) = refs[26:]

    me = lax.axis_index("dp")
    chips = n // CORES
    chip, core = me // CORES, lax.rem(me, CORES)
    partner = {"dp": chip * CORES + (1 - core)}
    ahead = {"dp": lax.rem(chip + 1, chips) * CORES + core}
    behind = {"dp": lax.rem(chip + chips - 1, chips) * CORES + core}
    layers = m[0].shape[0]

    def cut(layer):
        sizes = [x.shape[1] for x in m]
        parts = [(SLAB, sizes[0] - SLAB), (sizes[1],), (sizes[2] - TAIL, TAIL)]
        done = []
        for a, part in enumerate(parts):
            first = 0
            for count in part:
                if count > 0:
                    done.append((a, layer, first, count))
                first += count
        return done

    half = layers // 2
    there = [u for layer in range(half) for u in cut(layer)]
    back = [u for layer in range(half, layers) for u in cut(layer)]
    units = [u for pair in zip(there, back, strict=True) for u in pair]
    order = range(len(units))
    forward = [u % 2 == 0 for u in order]

    def rows(u, block, which):
        a, _, first, count = units[u]
        return pl.ds(pl.multiple_of((block * CORES + which) * m[a].shape[1] + first, SLAB), count)

    def slot(step, u):
        a, layer, first, count = units[u]
        part = pl.ds(first, count)
        return tall_slots.at[step, layer, part] if a == 2 else wide_slots.at[step, a * layers + layer, part]

    def w_own(u):
        a, layer, first, count = units[u]
        part = pl.ds(first, count)
        return tall_w.at[layer, part] if a == 2 else wide_w.at[a * layers + layer, part]

    def summed(step, u):
        return lax.rem(chip + 2 * chips - 1 - step, chips) if forward[u] else lax.rem(chip + 1 + step, chips)

    def gathered(step, u):
        return lax.rem(chip + chips - step, chips) if forward[u] else lax.rem(chip + step, chips)

    def remote(src, dst, send, recv, to):
        return pltpu.make_async_remote_copy(src_ref=src, dst_ref=dst, send_sem=send, recv_sem=recv, device_id=to, device_id_type=MESH)

    def load(step, u):
        a, layer, _, _ = units[u]
        mine = rows(u, summed(step, u), core)
        return pltpu.make_async_copy(g[a].at[0, layer, mine], whole[a].at[layer, mine], load_sem.at[step, u])

    def stage(u):
        a, layer, _, _ = units[u]
        return pltpu.make_async_copy(g[a].at[0, layer, rows(u, summed(0, u), 1 - core)], w_own(u), state_sem.at[0, u])

    def give(step, u, staged=False):
        a, layer, _, _ = units[u]
        block = summed(step, u)
        return remote(
            w_own(u) if staged else g[a].at[0, layer, rows(u, block, 1 - core)],
            whole[a].at[layer, rows(u, block, core)],
            give_send.at[step, u],
            give_recv.at[step, u],
            partner,
        )

    def send_sum(step, u):
        a, layer, _, _ = units[u]
        return remote(
            whole[a].at[layer, rows(u, summed(step, u), core)],
            slot(step, u),
            sum_send.at[step, u],
            sum_recv.at[step, u],
            ahead if forward[u] else behind,
        )

    def send_new(step, u):
        a, layer, _, _ = units[u]
        mine = whole[a].at[layer, rows(u, gathered(step, u), core)]
        return remote(mine, mine, new_send.at[step, u], new_recv.at[step, u], ahead if forward[u] else behind)

    def pass_new(step, u):
        a, layer, _, _ = units[u]
        mine = whole[a].at[layer, rows(u, gathered(step, u), core)]
        return remote(mine, mine, pass_send.at[step, u], pass_recv.at[step, u], partner)

    def state(u):
        a, layer, first, count = units[u]
        part = pl.ds(first, count)
        return (
            pltpu.make_async_copy(w[a].at[layer, rows(u, chip, core)], w_own(u), state_sem.at[0, u]),
            pltpu.make_async_copy(m_in[a].at[layer, part], m[a].at[layer, part], state_sem.at[1, u]),
            pltpu.make_async_copy(v_in[a].at[layer, part], v[a].at[layer, part], state_sem.at[2, u]),
        )

    for u in order:
        stage(u).start()
        load(0, u).start()
    barrier = pltpu.get_barrier_semaphore()
    for other in (partner, ahead, behind):
        pl.semaphore_signal(barrier, inc=1, device_id=other, device_id_type=MESH)
    pl.semaphore_wait(barrier, 3)
    for u in order:
        stage(u).wait()
        give(0, u, staged=True).start()

    def add(step, u, first=False, squared=None):
        a, layer, start, count = units[u]
        size = m[a].shape[1]
        block = summed(step, u)
        load(step, u).wait()
        give(step, u).wait_recv()
        if not first:
            send_sum(step - 1, u).wait_recv()
        mine, other = (block * CORES + core) * size + start, (block * CORES + 1 - core) * size + start

        def body(i, squared):
            at = pl.ds(pl.multiple_of(mine + i * SLAB, SLAB), SLAB)
            total = whole[a][layer, at, :].astype(jnp.float32)
            total += whole[a][layer, pl.ds(pl.multiple_of(other + i * SLAB, SLAB), SLAB), :].astype(jnp.float32)
            if not first:
                total = slot(step - 1, u)[pl.ds(pl.multiple_of(i * SLAB, SLAB), SLAB), :].astype(jnp.float32) + total
            total = total.astype(jnp.bfloat16)
            whole[a][layer, at, :] = total
            if want is None:
                return 0
            total = total.astype(jnp.float32)
            total = total * total
            pieces = [total[r : r + 8, k : k + 128] for r in range(0, SLAB, 8) for k in range(0, total.shape[1], 128)]
            while len(pieces) > 1:
                pieces = [sum(pieces[k : k + 2]) for k in range(0, len(pieces), 2)]
            return squared + pieces[0]

        want = squared
        return lax.fori_loop(0, count // SLAB, body, 0 if want is None else want)

    def add_and_send(step, u, first=False):
        add(step, u, first)
        send_sum(step, u).start()

    def prefetch(step):
        for u in order:
            load(step, u).start()
            give(step, u).start()

    prefetch(1)
    for u in order:
        add_and_send(0, u, first=True)
    for u in order:
        give(0, u, staged=True).wait_send()
        for copy in state(u):
            copy.start()

    def middle(step, carry):
        prefetch(step + 1)
        for u in order:
            add_and_send(step, u)
        for u in order:
            send_sum(step - 1, u).wait_send()
            give(step, u).wait_send()
        return carry

    lax.fori_loop(1, chips - 1, middle, 0)

    total = jnp.zeros((8, 128), jnp.float32)
    for u in order:
        total = add(chips - 1, u, squared=total)
        send_sum(chips - 2, u).wait_send()

    squares[me] = jnp.sum(total, axis=0, keepdims=True)

    def norm(k):
        return remote(squares.at[me], squares.at[me], norm_send.at[k], norm_recv.at[k], {"dp": lax.rem(me + k, n)})

    for k in range(1, n):
        norm(k).start()
    for u in order:
        give(chips - 1, u).wait_send()
        for copy in state(u):
            copy.wait()
    for k in range(1, n):
        norm(k).wait_recv()
    every = jnp.sum(jnp.sum(squares[...], axis=0), axis=1, keepdims=True)
    count = n * sum(one.size for one in m)
    factor = jnp.minimum(1.0, 0.5 * lax.rsqrt(every / count + 1e-30))

    for u in order:
        a, layer, first, count = units[u]
        base = me * m[a].shape[1] + first

        def body(i, carry, a=a, layer=layer, u=u, base=base, first=first):
            at = pl.ds(pl.multiple_of(first + i * SLAB, SLAB), SLAB)
            mine = pl.ds(pl.multiple_of(base + i * SLAB, SLAB), SLAB)
            gradient = whole[a][layer, mine, :].astype(jnp.float32) * factor
            weight = w_own(u)[pl.ds(pl.multiple_of(i * SLAB, SLAB), SLAB), :].astype(jnp.float32)
            moment = 0.9 * m[a][layer, at, :] + 0.1 * gradient
            second = 0.95 * v[a][layer, at, :] + 0.05 * gradient * gradient
            m[a][layer, at, :] = moment
            v[a][layer, at, :] = second
            change = moment * lax.rsqrt(second + 1e-8) + 0.1 * weight
            whole[a][layer, mine, :] = (weight - 0.02 * change).astype(jnp.bfloat16)
            return carry

        lax.fori_loop(0, count // SLAB, body, 0)
        send_new(0, u).start()
        pass_new(0, u).start()

    def onward(step, carry):
        for u in order:
            send_new(step - 1, u).wait_recv()
            send_new(step, u).start()
            pass_new(step, u).start()
        for u in order:
            send_new(step - 1, u).wait_send()
            pass_new(step - 1, u).wait()
        return carry

    lax.fori_loop(1, chips - 1, onward, 0)
    for u in order:
        send_new(chips - 2, u).wait_recv()
        pass_new(chips - 1, u).start()
    for k in range(1, n):
        norm(k).wait_send()
    for u in order:
        send_new(chips - 2, u).wait_send()
        pass_new(chips - 2, u).wait()
    for u in order:
        pass_new(chips - 1, u).wait()


def write_out(*refs):
    count = (len(refs) - 1) // 2
    copies = []
    for src, dst in zip(refs[:count], refs[count:-1], strict=True):
        for layer in range(src.shape[0]):
            copies.append(pltpu.make_async_copy(src.at[layer], dst.at[layer], refs[-1].at[len(copies)]))
    for copy in copies:
        copy.start()
    for copy in copies:
        copy.wait()


def solution(mesh):
    n = mesh.shape["dp"]
    chips = n // CORES

    def step(*arrays):
        weights, m, v = (arrays[i : i + 3] for i in (3, 6, 9))
        layers, wide, columns = m[0].shape
        _, tall, narrow = m[2].shape
        unit = layers * PIECES
        whole = [pltpu.VMEM(x.shape, x.dtype) for x in weights]
        moments = [pltpu.VMEM(x.shape, x.dtype) for x in (*m, *v)]
        dma = pltpu.SemaphoreType.DMA
        done = pl.pallas_call(
            functools.partial(kernel, n),
            out_shape=[*whole, *moments],
            in_specs=[pl.BlockSpec(memory_space=pltpu.HBM)] * 12,
            out_specs=[pl.BlockSpec(memory_space=pltpu.VMEM)] * 9,
            scratch_shapes=[
                pltpu.VMEM((chips - 1, 2 * layers, wide, columns), jnp.bfloat16),
                pltpu.VMEM((chips - 1, layers, tall, narrow), jnp.bfloat16),
                pltpu.VMEM((2 * layers, wide, columns), jnp.bfloat16),
                pltpu.VMEM((layers, tall, narrow), jnp.bfloat16),
                pltpu.VMEM((n, 1, 128), jnp.float32),
                dma((chips, unit)),
                dma((chips, unit)),
                dma((chips, unit)),
                dma((chips - 1, unit)),
                dma((chips - 1, unit)),
                dma((3, unit)),
                dma((n,)),
                dma((n,)),
                dma((chips - 1, unit)),
                dma((chips - 1, unit)),
                dma((chips, unit)),
                dma((chips, unit)),
            ],
            compiler_params=pltpu.CompilerParams(collective_id=0, has_side_effects=True, vmem_limit_bytes=VMEM_LIMIT),
            name="clipped_step",
        )(*arrays)

        def out(*xs):
            return pl.pallas_call(
                write_out,
                out_shape=[jax.ShapeDtypeStruct(x.shape, x.dtype) for x in xs],
                in_specs=[pl.BlockSpec(memory_space=pltpu.VMEM)] * len(xs),
                out_specs=[pl.BlockSpec(memory_space=pltpu.HBM)] * len(xs),
                scratch_shapes=[dma((len(xs) * layers,))],
                compiler_params=pltpu.CompilerParams(vmem_limit_bytes=VMEM_LIMIT),
                name="write_out",
            )(*xs)

        moments = out(*done[3:])
        return (*out(*done[:3]), *moments)

    all_of, cut = P(None, None, None), P(None, "dp", None)
    return jax.shard_map(
        step,
        mesh=mesh,
        in_specs=(P(("rep", "dp"), None, None, None),) * 3 + (all_of,) * 3 + (cut,) * 6,
        out_specs=(P("rep", None, None),) * 3 + (P("rep", "dp", None),) * 6,
        check_vma=False,
    )
```

time: 368 us -> 367 us (level)
    pallas_call x4 -> x2, Pallas kernels: 16.5 us -> 14.9 us  [out(): pl.pallas_call(write_out, out_shape=[jax.ShapeDtypeStruct(x.shape, x.dtyp...]
where the time goes in v2:
time: 367 us
  Pallas kernels  366 us (100%)
    pallas_call x1, Pallas kernels, step(): pl.pallas_call(functools.partial(kernel, n), out_shape=[*whole, *moments]...  351 us
    pallas_call x2, Pallas kernels, out(): pl.pallas_call(write_out, out_shape=[jax.ShapeDtypeStruct(x.shape, x.dtyp...  14.9 us

profile of v2, /device:TPU:21, one launch (start us, length us, event | category | flops | bytes accessed | tf_op | source)
XLA Modules:
  0.0 366.7 jit_solution(430824702376961751)
XLA Ops:
  0.6 351.1 %clipped_step.1 = (bf16[2,1024,2816]{2,1,0:T(8,128)(2,1)S(1)}, bf16[2,1024,2816]{2,1,0:T(8,128)(2,1)S(1)}, bf16[2,2816,1024]{2,1,0:T(8,128)(2,1)S(1)}, f32[2,64,...) custom-call(bf16[1,2,1024,2816]{3,2,1,0:T(8,128)(2,1)} %refs_0_.1, ...), custom_call_target="tpu_custom_call" | custom-call | tf_op jit(solution)/shard_map/clipped_step/pallas_call | solution.py:282
  351.8 11.4 %write_out.2 = (bf16[2,1024,2816]{2,1,0:T(8,128)(2,1)}, bf16[2,1024,2816]{2,1,0:T(8,128)(2,1)}, bf16[2,2816,1024]{2,1,0:T(8,128)(2,1)}) custom-call(bf16[2,1024,2816]{2,1,0:T(8,128)(2,1)S(1)} %get-tuple-element.27.refs_0_, bf16[2,1024,2816]{2,1,0:T(8,128)(2,1)S(1)} %get-tuple-element.28.refs_1_, bf16[2,2816,1024]{2,1,0:T(8,128)(2,1)S(1)} %get-tuple-element.29.refs_2_), custom_call_target="tpu_custom_call" | custom-call | tf_op jit(solution)/shard_map/write_out/pallas_call | solution.py:311
  363.2 3.5 write_out.3

commit v3 on v2

--- a/solution.py
+++ b/solution.py
@@ -19,7 +19,7 @@
     g, w, m_in, v_in = refs[0:3], refs[3:6], refs[6:9], refs[9:12]
     whole, m, v = refs[12:15], refs[15:18], refs[18:21]
     wide_slots, tall_slots, wide_w, tall_w, squares = refs[21:26]
-    (load_sem, give_send, give_recv, sum_send, sum_recv, state_sem, norm_send, norm_recv, new_send, new_recv, pass_send, pass_recv) = refs[26:]
+    load_sem, across_send, across_recv, ring_send, ring_recv, w_sem, moment_sem, norm_send, norm_recv = refs[26:]
 
     me = lax.axis_index("dp")
     chips = n // CORES
@@ -71,14 +71,17 @@
     def remote(src, dst, send, recv, to):
         return pltpu.make_async_remote_copy(src_ref=src, dst_ref=dst, send_sem=send, recv_sem=recv, device_id=to, device_id_type=MESH)
 
+    def turn(step):
+        return step % 2 if isinstance(step, int) else lax.rem(step, 2)
+
     def load(step, u):
         a, layer, _, _ = units[u]
         mine = rows(u, summed(step, u), core)
-        return pltpu.make_async_copy(g[a].at[0, layer, mine], whole[a].at[layer, mine], load_sem.at[step, u])
+        return pltpu.make_async_copy(g[a].at[0, layer, mine], whole[a].at[layer, mine], load_sem.at[turn(step), u])
 
     def stage(u):
         a, layer, _, _ = units[u]
-        return pltpu.make_async_copy(g[a].at[0, layer, rows(u, summed(0, u), 1 - core)], w_own(u), state_sem.at[0, u])
+        return pltpu.make_async_copy(g[a].at[0, layer, rows(u, summed(0, u), 1 - core)], w_own(u), load_sem.at[1, u])
 
     def give(step, u, staged=False):
         a, layer, _, _ = units[u]
@@ -86,8 +89,8 @@
         return remote(
             w_own(u) if staged else g[a].at[0, layer, rows(u, block, 1 - core)],
             whole[a].at[layer, rows(u, block, core)],
-            give_send.at[step, u],
-            give_recv.at[step, u],
+            across_send.at[turn(step), u],
+            across_recv.at[step, u],
             partner,
         )
 
@@ -96,38 +99,49 @@
         return remote(
             whole[a].at[layer, rows(u, summed(step, u), core)],
             slot(step, u),
-            sum_send.at[step, u],
-            sum_recv.at[step, u],
+            ring_send.at[turn(step), u],
+            ring_recv.at[step, u],
             ahead if forward[u] else behind,
         )
 
     def send_new(step, u):
         a, layer, _, _ = units[u]
         mine = whole[a].at[layer, rows(u, gathered(step, u), core)]
-        return remote(mine, mine, new_send.at[step, u], new_recv.at[step, u], ahead if forward[u] else behind)
+        return remote(mine, mine, ring_send.at[turn(step), u], ring_recv.at[step, u], ahead if forward[u] else behind)
 
     def pass_new(step, u):
         a, layer, _, _ = units[u]
         mine = whole[a].at[layer, rows(u, gathered(step, u), core)]
-        return remote(mine, mine, pass_send.at[step, u], pass_recv.at[step, u], partner)
-
-    def state(u):
-        a, layer, first, count = units[u]
-        part = pl.ds(first, count)
+        return remote(mine, mine, across_send.at[turn(step), u], across_recv.at[step, u], partner)
+
+    def own_weights(u):
+        a, layer, _, _ = units[u]
+        return pltpu.make_async_copy(w[a].at[layer, rows(u, chip, core)], w_own(u), w_sem.at[u])
+
+    def moments(a):
         return (
-            pltpu.make_async_copy(w[a].at[layer, rows(u, chip, core)], w_own(u), state_sem.at[0, u]),
-            pltpu.make_async_copy(m_in[a].at[layer, part], m[a].at[layer, part], state_sem.at[1, u]),
-            pltpu.make_async_copy(v_in[a].at[layer, part], v[a].at[layer, part], state_sem.at[2, u]),
+            pltpu.make_async_copy(m_in[a], m[a], moment_sem.at[0, a]),
+            pltpu.make_async_copy(v_in[a], v[a], moment_sem.at[1, a]),
         )
 
-    for u in order:
+    def fetch(u):
         stage(u).start()
         load(0, u).start()
+
+    first_of_each, rest = order[:2], order[2:]
+    for u in first_of_each:
+        fetch(u)
     barrier = pltpu.get_barrier_semaphore()
     for other in (partner, ahead, behind):
         pl.semaphore_signal(barrier, inc=1, device_id=other, device_id_type=MESH)
+    for u in rest:
+        fetch(u)
+    for u in first_of_each:
+        stage(u).wait()
     pl.semaphore_wait(barrier, 3)
-    for u in order:
+    for u in first_of_each:
+        give(0, u, staged=True).start()
+    for u in rest:
         stage(u).wait()
         give(0, u, staged=True).start()
 
@@ -161,37 +175,42 @@
         want = squared
         return lax.fori_loop(0, count // SLAB, body, 0 if want is None else want)
 
-    def add_and_send(step, u, first=False):
-        add(step, u, first)
-        send_sum(step, u).start()
-
-    def prefetch(step):
+    def fetch_next(step):
         for u in order:
-            load(step, u).start()
-            give(step, u).start()
-
-    prefetch(1)
-    for u in order:
-        add_and_send(0, u, first=True)
-    for u in order:
-        give(0, u, staged=True).wait_send()
-        for copy in state(u):
+            load(step + 1, u).start()
+            if not isinstance(step, int) or step > 0:
+                give(step - 1, u).wait_send()
+            give(step + 1, u).start()
+
+    for u in order:
+        add(0, u, first=True)
+        send_sum(0, u).start()
+    fetch_next(0)
+    fetch_next(1)
+    for u in order:
+        add(1, u)
+        send_sum(1, u).start()
+    for u in order:
+        own_weights(u).start()
+    for a in range(3):
+        for copy in moments(a):
             copy.start()
 
     def middle(step, carry):
-        prefetch(step + 1)
+        fetch_next(step)
         for u in order:
-            add_and_send(step, u)
-        for u in order:
-            send_sum(step - 1, u).wait_send()
-            give(step, u).wait_send()
+            add(step, u)
+            send_sum(step - 2, u).wait_send()
+            send_sum(step, u).start()
         return carry
 
-    lax.fori_loop(1, chips - 1, middle, 0)
+    lax.fori_loop(2, chips - 1, middle, 0)
 
     total = jnp.zeros((8, 128), jnp.float32)
     for u in order:
         total = add(chips - 1, u, squared=total)
+    for u in order:
+        send_sum(chips - 3, u).wait_send()
         send_sum(chips - 2, u).wait_send()
 
     squares[me] = jnp.sum(total, axis=0, keepdims=True)
@@ -199,11 +218,14 @@
     def norm(k):
         return remote(squares.at[me], squares.at[me], norm_send.at[k], norm_recv.at[k], {"dp": lax.rem(me + k, n)})
 
-    for k in range(1, n):
+    for k in sorted(range(1, n), key=lambda k: abs(k - n // 2)):
         norm(k).start()
     for u in order:
+        give(chips - 2, u).wait_send()
         give(chips - 1, u).wait_send()
-        for copy in state(u):
+        own_weights(u).wait()
+    for a in range(3):
+        for copy in moments(a):
             copy.wait()
     for k in range(1, n):
         norm(k).wait_recv()
@@ -232,23 +254,31 @@
         send_new(0, u).start()
         pass_new(0, u).start()
 
-    def onward(step, carry):
+    def onward(step, u):
+        send_new(step - 1, u).wait_recv()
+        if not isinstance(step, int) or step > 1:
+            send_new(step - 2, u).wait_send()
+            pass_new(step - 2, u).wait()
+        send_new(step, u).start()
+        pass_new(step, u).start()
+
+    for u in order:
+        onward(1, u)
+
+    def later(step, carry):
         for u in order:
-            send_new(step - 1, u).wait_recv()
-            send_new(step, u).start()
-            pass_new(step, u).start()
-        for u in order:
-            send_new(step - 1, u).wait_send()
-            pass_new(step - 1, u).wait()
+            onward(step, u)
         return carry
 
-    lax.fori_loop(1, chips - 1, onward, 0)
+    lax.fori_loop(2, chips - 1, later, 0)
     for u in order:
         send_new(chips - 2, u).wait_recv()
+        pass_new(chips - 3, u).wait()
         pass_new(chips - 1, u).start()
     for k in range(1, n):
         norm(k).wait_send()
     for u in order:
+        send_new(chips - 3, u).wait_send()
         send_new(chips - 2, u).wait_send()
         pass_new(chips - 2, u).wait()
     for u in order:
@@ -277,11 +307,11 @@
         _, tall, narrow = m[2].shape
         unit = layers * PIECES
         whole = [pltpu.VMEM(x.shape, x.dtype) for x in weights]
-        moments = [pltpu.VMEM(x.shape, x.dtype) for x in (*m, *v)]
+        states = [pltpu.VMEM(x.shape, x.dtype) for x in (*m, *v)]
         dma = pltpu.SemaphoreType.DMA
         done = pl.pallas_call(
             functools.partial(kernel, n),
-            out_shape=[*whole, *moments],
+            out_shape=[*whole, *states],
             in_specs=[pl.BlockSpec(memory_space=pltpu.HBM)] * 12,
             out_specs=[pl.BlockSpec(memory_space=pltpu.VMEM)] * 9,
             scratch_shapes=[
@@ -290,18 +320,15 @@
                 pltpu.VMEM((2 * layers, wide, columns), jnp.bfloat16),
                 pltpu.VMEM((layers, tall, narrow), jnp.bfloat16),
                 pltpu.VMEM((n, 1, 128), jnp.float32),
+                dma((2, unit)),
+                dma((2, unit)),
                 dma((chips, unit)),
-                dma((chips, unit)),
-                dma((chips, unit)),
+                dma((2, unit)),
                 dma((chips - 1, unit)),
-                dma((chips - 1, unit)),
-                dma((3, unit)),
+                dma((unit,)),
+                dma((2, 3)),
                 dma((n,)),
                 dma((n,)),
-                dma((chips - 1, unit)),
-                dma((chips - 1, unit)),
-                dma((chips, unit)),
-                dma((chips, unit)),
             ],
             compiler_params=pltpu.CompilerParams(collective_id=0, has_side_effects=True, vmem_limit_bytes=VMEM_LIMIT),
             name="clipped_step",
@@ -318,8 +345,7 @@
                 name="write_out",
             )(*xs)
 
-        moments = out(*done[3:])
-        return (*out(*done[:3]), *moments)
+        return (*out(*done[:3]), *out(*done[3:]))
 
     all_of, cut = P(None, None, None), P(None, "dp", None)
     return jax.shard_map(

time: 367 us -> 362 us (0.986)
  Pallas kernels: 366 us -> 361 us
    pallas_call x1, Pallas kernels: 351 us -> 347 us  [step(): pl.pallas_call(functools.partial(kernel, n), out_shape=[*whole, *states],...]
where the time goes in v3:
time: 362 us
  Pallas kernels  361 us (100%)
    pallas_call x1, Pallas kernels, step(): pl.pallas_call(functools.partial(kernel, n), out_shape=[*whole, *states],...  347 us
    pallas_call x2, Pallas kernels, out(): pl.pallas_call(write_out, out_shape=[jax.ShapeDtypeStruct(x.shape, x.dtyp...  14.9 us

profile of v3, /device:TPU:21, one launch (start us, length us, event | category | flops | bytes accessed | tf_op | source)
XLA Modules:
  0.0 362.2 jit_solution(10578625079130478124)
XLA Ops:
  0.6 346.6 %clipped_step.1 = (bf16[2,1024,2816]{2,1,0:T(8,128)(2,1)S(1)}, bf16[2,1024,2816]{2,1,0:T(8,128)(2,1)S(1)}, bf16[2,2816,1024]{2,1,0:T(8,128)(2,1)S(1)}, f32[2,64,...) custom-call(bf16[1,2,1024,2816]{3,2,1,0:T(8,128)(2,1)} %refs_0_.1, ...), custom_call_target="tpu_custom_call" | custom-call | tf_op jit(solution)/shard_map/clipped_step/pallas_call | solution.py:312
  347.3 11.4 %write_out.2 = (bf16[2,1024,2816]{2,1,0:T(8,128)(2,1)}, bf16[2,1024,2816]{2,1,0:T(8,128)(2,1)}, bf16[2,2816,1024]{2,1,0:T(8,128)(2,1)}) custom-call(bf16[2,1024,2816]{2,1,0:T(8,128)(2,1)S(1)} %get-tuple-element.27.refs_0_, bf16[2,1024,2816]{2,1,0:T(8,128)(2,1)S(1)} %get-tuple-element.28.refs_1_, bf16[2,2816,1024]{2,1,0:T(8,128)(2,1)S(1)} %get-tuple-element.29.refs_2_), custom_call_target="tpu_custom_call" | custom-call | tf_op jit(solution)/shard_map/write_out/pallas_call | solution.py:338
  358.7 3.5 write_out.3

commit v4 on v3

--- a/solution.py
+++ b/solution.py
@@ -12,6 +12,7 @@
 SLAB = 16
 TAIL = 48
 PIECES = 5
+PARTS = 4
 VMEM_LIMIT = 18 * 2**20
 
 
@@ -19,7 +20,7 @@
     g, w, m_in, v_in = refs[0:3], refs[3:6], refs[6:9], refs[9:12]
     whole, m, v = refs[12:15], refs[15:18], refs[18:21]
     wide_slots, tall_slots, wide_w, tall_w, squares = refs[21:26]
-    load_sem, across_send, across_recv, ring_send, ring_recv, w_sem, moment_sem, norm_send, norm_recv = refs[26:]
+    load_sem, across_send, across_recv, ring_send, ring_recv, moment_sem, norm_send, norm_recv = refs[26:]
 
     me = lax.axis_index("dp")
     chips = n // CORES
@@ -89,7 +90,7 @@
         return remote(
             w_own(u) if staged else g[a].at[0, layer, rows(u, block, 1 - core)],
             whole[a].at[layer, rows(u, block, core)],
-            across_send.at[turn(step), u],
+            across_send.at[u],
             across_recv.at[step, u],
             partner,
         )
@@ -99,7 +100,7 @@
         return remote(
             whole[a].at[layer, rows(u, summed(step, u), core)],
             slot(step, u),
-            ring_send.at[turn(step), u],
+            ring_send.at[u],
             ring_recv.at[step, u],
             ahead if forward[u] else behind,
         )
@@ -107,16 +108,16 @@
     def send_new(step, u):
         a, layer, _, _ = units[u]
         mine = whole[a].at[layer, rows(u, gathered(step, u), core)]
-        return remote(mine, mine, ring_send.at[turn(step), u], ring_recv.at[step, u], ahead if forward[u] else behind)
+        return remote(mine, mine, ring_send.at[u], ring_recv.at[step, u], ahead if forward[u] else behind)
 
     def pass_new(step, u):
         a, layer, _, _ = units[u]
         mine = whole[a].at[layer, rows(u, gathered(step, u), core)]
-        return remote(mine, mine, across_send.at[turn(step), u], across_recv.at[step, u], partner)
+        return remote(mine, mine, across_send.at[u], across_recv.at[step, u], partner)
 
     def own_weights(u):
         a, layer, _, _ = units[u]
-        return pltpu.make_async_copy(w[a].at[layer, rows(u, chip, core)], w_own(u), w_sem.at[u])
+        return pltpu.make_async_copy(w[a].at[layer, rows(u, chip, core)], w_own(u), load_sem.at[turn(chips), u])
 
     def moments(a):
         return (
@@ -178,20 +179,13 @@
     def fetch_next(step):
         for u in order:
             load(step + 1, u).start()
-            if not isinstance(step, int) or step > 0:
-                give(step - 1, u).wait_send()
+            give(step, u).wait_send()
             give(step + 1, u).start()
 
     for u in order:
         add(0, u, first=True)
         send_sum(0, u).start()
     fetch_next(0)
-    fetch_next(1)
-    for u in order:
-        add(1, u)
-        send_sum(1, u).start()
-    for u in order:
-        own_weights(u).start()
     for a in range(3):
         for copy in moments(a):
             copy.start()
@@ -200,17 +194,18 @@
         fetch_next(step)
         for u in order:
             add(step, u)
-            send_sum(step - 2, u).wait_send()
+            send_sum(step - 1, u).wait_send()
             send_sum(step, u).start()
         return carry
 
-    lax.fori_loop(2, chips - 1, middle, 0)
+    lax.fori_loop(1, chips - 1, middle, 0)
+    for u in order:
+        own_weights(u).start()
 
     total = jnp.zeros((8, 128), jnp.float32)
     for u in order:
         total = add(chips - 1, u, squared=total)
     for u in order:
-        send_sum(chips - 3, u).wait_send()
         send_sum(chips - 2, u).wait_send()
 
     squares[me] = jnp.sum(total, axis=0, keepdims=True)
@@ -221,7 +216,6 @@
     for k in sorted(range(1, n), key=lambda k: abs(k - n // 2)):
         norm(k).start()
     for u in order:
-        give(chips - 2, u).wait_send()
         give(chips - 1, u).wait_send()
         own_weights(u).wait()
     for a in range(3):
@@ -255,32 +249,27 @@
         pass_new(0, u).start()
 
     def onward(step, u):
-        send_new(step - 1, u).wait_recv()
-        if not isinstance(step, int) or step > 1:
-            send_new(step - 2, u).wait_send()
-            pass_new(step - 2, u).wait()
+        send_new(step - 1, u).wait()
+        pass_new(step - 1, u).wait_send()
         send_new(step, u).start()
         pass_new(step, u).start()
-
-    for u in order:
-        onward(1, u)
 
     def later(step, carry):
         for u in order:
             onward(step, u)
+        for u in order:
+            pass_new(step - 1, u).wait_recv()
         return carry
 
-    lax.fori_loop(2, chips - 1, later, 0)
-    for u in order:
-        send_new(chips - 2, u).wait_recv()
-        pass_new(chips - 3, u).wait()
+    lax.fori_loop(1, chips - 1, later, 0)
+    for u in order:
+        send_new(chips - 2, u).wait()
+        pass_new(chips - 2, u).wait_send()
         pass_new(chips - 1, u).start()
     for k in range(1, n):
         norm(k).wait_send()
     for u in order:
-        send_new(chips - 3, u).wait_send()
-        send_new(chips - 2, u).wait_send()
-        pass_new(chips - 2, u).wait()
+        pass_new(chips - 2, u).wait_recv()
     for u in order:
         pass_new(chips - 1, u).wait()
 
@@ -289,8 +278,12 @@
     count = (len(refs) - 1) // 2
     copies = []
     for src, dst in zip(refs[:count], refs[count:-1], strict=True):
+        parts = PARTS if src.dtype == jnp.bfloat16 else 1
+        size = src.shape[1] // parts
         for layer in range(src.shape[0]):
-            copies.append(pltpu.make_async_copy(src.at[layer], dst.at[layer], refs[-1].at[len(copies)]))
+            for part in range(parts):
+                at = layer, pl.ds(part * size, size)
+                copies.append(pltpu.make_async_copy(src.at[at], dst.at[at], refs[-1].at[len(copies)]))
     for copy in copies:
         copy.start()
     for copy in copies:
@@ -321,11 +314,10 @@
                 pltpu.VMEM((layers, tall, narrow), jnp.bfloat16),
                 pltpu.VMEM((n, 1, 128), jnp.float32),
                 dma((2, unit)),
-                dma((2, unit)),
+                dma((unit,)),
                 dma((chips, unit)),
-                dma((2, unit)),
+                dma((unit,)),
                 dma((chips - 1, unit)),
-                dma((unit,)),
                 dma((2, 3)),
                 dma((n,)),
                 dma((n,)),
@@ -340,7 +332,7 @@
                 out_shape=[jax.ShapeDtypeStruct(x.shape, x.dtype) for x in xs],
                 in_specs=[pl.BlockSpec(memory_space=pltpu.VMEM)] * len(xs),
                 out_specs=[pl.BlockSpec(memory_space=pltpu.HBM)] * len(xs),
-                scratch_shapes=[dma((len(xs) * layers,))],
+                scratch_shapes=[dma((sum(layers * (PARTS if x.dtype == jnp.bfloat16 else 1) for x in xs),))],
                 compiler_params=pltpu.CompilerParams(vmem_limit_bytes=VMEM_LIMIT),
                 name="write_out",
             )(*xs)

time: 362 us -> 362 us (level)
  no operation moved by 1% of the time
where the time goes in v4:
time: 362 us
  Pallas kernels  361 us (100%)
    pallas_call x1, Pallas kernels, step(): pl.pallas_call(functools.partial(kernel, n), out_shape=[*whole, *states],...  346 us
    pallas_call x2, Pallas kernels, out(): pl.pallas_call(write_out, out_shape=[jax.ShapeDtypeStruct(x.shape, x.dtyp...  14.9 us

profile of v4, /device:TPU:21, one launch (start us, length us, event | category | flops | bytes accessed | tf_op | source)
XLA Modules:
  0.0 361.9 jit_solution(6969288259361028833)
XLA Ops:
  0.6 346.3 %clipped_step.1 = (bf16[2,1024,2816]{2,1,0:T(8,128)(2,1)S(1)}, bf16[2,1024,2816]{2,1,0:T(8,128)(2,1)S(1)}, bf16[2,2816,1024]{2,1,0:T(8,128)(2,1)S(1)}, f32[2,64,...) custom-call(bf16[1,2,1024,2816]{3,2,1,0:T(8,128)(2,1)} %refs_0_.1, ...), custom_call_target="tpu_custom_call" | custom-call | tf_op jit(solution)/shard_map/clipped_step/pallas_call | solution.py:305
  347.0 11.4 %write_out.2 = (bf16[2,1024,2816]{2,1,0:T(8,128)(2,1)}, bf16[2,1024,2816]{2,1,0:T(8,128)(2,1)}, bf16[2,2816,1024]{2,1,0:T(8,128)(2,1)}) custom-call(bf16[2,1024,2816]{2,1,0:T(8,128)(2,1)S(1)} %get-tuple-element.27.refs_0_, bf16[2,1024,2816]{2,1,0:T(8,128)(2,1)S(1)} %get-tuple-element.28.refs_1_, bf16[2,2816,1024]{2,1,0:T(8,128)(2,1)S(1)} %get-tuple-element.29.refs_2_), custom_call_target="tpu_custom_call" | custom-call | tf_op jit(solution)/shard_map/write_out/pallas_call | solution.py:330
  358.4 3.5 write_out.3

commit v5 on v4

--- a/solution.py
+++ b/solution.py
@@ -20,7 +20,7 @@
     g, w, m_in, v_in = refs[0:3], refs[3:6], refs[6:9], refs[9:12]
     whole, m, v = refs[12:15], refs[15:18], refs[18:21]
     wide_slots, tall_slots, wide_w, tall_w, squares = refs[21:26]
-    load_sem, across_send, across_recv, ring_send, ring_recv, moment_sem, norm_send, norm_recv = refs[26:]
+    load_sem, across_send, across_recv, ring_send, ring_recv, moment_sem, norm_recv = refs[26:]
 
     me = lax.axis_index("dp")
     chips = n // CORES
@@ -210,8 +210,10 @@
 
     squares[me] = jnp.sum(total, axis=0, keepdims=True)
 
+    free = [ring_send.at[u] for u in order] + [load_sem.at[turn(chips - 1), u] for u in order]
+
     def norm(k):
-        return remote(squares.at[me], squares.at[me], norm_send.at[k], norm_recv.at[k], {"dp": lax.rem(me + k, n)})
+        return remote(squares.at[me], squares.at[me], free[k - 1], norm_recv.at[k], {"dp": lax.rem(me + k, n)})
 
     for k in sorted(range(1, n), key=lambda k: abs(k - n // 2)):
         norm(k).start()
@@ -222,7 +224,7 @@
         for copy in moments(a):
             copy.wait()
     for k in range(1, n):
-        norm(k).wait_recv()
+        norm(k).wait()
     every = jnp.sum(jnp.sum(squares[...], axis=0), axis=1, keepdims=True)
     count = n * sum(one.size for one in m)
     factor = jnp.minimum(1.0, 0.5 * lax.rsqrt(every / count + 1e-30))
@@ -266,8 +268,6 @@
         send_new(chips - 2, u).wait()
         pass_new(chips - 2, u).wait_send()
         pass_new(chips - 1, u).start()
-    for k in range(1, n):
-        norm(k).wait_send()
     for u in order:
         pass_new(chips - 2, u).wait_recv()
     for u in order:
@@ -320,7 +320,6 @@
                 dma((chips - 1, unit)),
                 dma((2, 3)),
                 dma((n,)),
-                dma((n,)),
             ],
             compiler_params=pltpu.CompilerParams(collective_id=0, has_side_effects=True, vmem_limit_bytes=VMEM_LIMIT),
             name="clipped_step",

time: 362 us -> 362 us (level)
  no operation moved by 1% of the time
where the time goes in v5:
time: 362 us
  Pallas kernels  361 us (100%)
    pallas_call x1, Pallas kernels, step(): pl.pallas_call(functools.partial(kernel, n), out_shape=[*whole, *states],...  346 us
    pallas_call x2, Pallas kernels, out(): pl.pallas_call(write_out, out_shape=[jax.ShapeDtypeStruct(x.shape, x.dtyp...  14.9 us

profile of v5, /device:TPU:21, one launch (start us, length us, event | category | flops | bytes accessed | tf_op | source)
XLA Modules:
  0.0 361.7 jit_solution(9172658974328217527)
XLA Ops:
  0.6 346.2 %clipped_step.1 = (bf16[2,1024,2816]{2,1,0:T(8,128)(2,1)S(1)}, bf16[2,1024,2816]{2,1,0:T(8,128)(2,1)S(1)}, bf16[2,2816,1024]{2,1,0:T(8,128)(2,1)S(1)}, f32[2,64,...) custom-call(bf16[1,2,1024,2816]{3,2,1,0:T(8,128)(2,1)} %refs_0_.1, ...), custom_call_target="tpu_custom_call" | custom-call | tf_op jit(solution)/shard_map/clipped_step/pallas_call | solution.py:305
  346.8 11.4 %write_out.2 = (bf16[2,1024,2816]{2,1,0:T(8,128)(2,1)}, bf16[2,1024,2816]{2,1,0:T(8,128)(2,1)}, bf16[2,2816,1024]{2,1,0:T(8,128)(2,1)}) custom-call(bf16[2,1024,2816]{2,1,0:T(8,128)(2,1)S(1)} %get-tuple-element.27.refs_0_, bf16[2,1024,2816]{2,1,0:T(8,128)(2,1)S(1)} %get-tuple-element.28.refs_1_, bf16[2,2816,1024]{2,1,0:T(8,128)(2,1)S(1)} %get-tuple-element.29.refs_2_), custom_call_target="tpu_custom_call" | custom-call | tf_op jit(solution)/shard_map/write_out/pallas_call | solution.py:329
  358.3 3.5 write_out.3
